TPU v7x, 32 devices: a whole 2x2x4 slice. The times are simulated.
32 devices in a mesh: grp: 2 (over x), pix: 16 (over z, y, core).
Axes of the slice: x: 2, y: 2, z: 4, core: 2. Of those that a mesh axis runs over, the one named last changes fastest.
Arguments:
- slcs: bfloat16 [2, 2048, 2048], P(None, ('grp', 'pix')), parts along dimension 1, may hold values from -6 to 6
- ref_date: int32 [2], P('grp'), parts along dimension 0, may hold values from 0 to 15
Outputs:
- spectrum: float32 [2, 2048, 2048], P(None, ('grp', 'pix')), parts along dimension 1
- compressed: float32 [2, 64, 4096], P(None, None, ('grp', 'pix')), parts along dimension 2
There are 2 independent parts, one for each index of `grp`. A program takes and returns all parts, laid end to end along the dimension named above; each array names one. Nothing has to cross between parts.
All inputs are finite; a program needn't handle non-finite values.
Results may differ from a plain program's by a relative error of at most 0.0057.
Values may be sent and summed in bfloat16 or wider, within the bound.
A program may use at most 64 MiB of HBM per device.

v0:
```python
import math

import jax
import jax.numpy as jnp
from jax import lax
from jax.sharding import PartitionSpec as P

DATES = 16
ROWS = 64
HALF_X = 5
HALF_Y = 2
POWER_ITERS = 6


LOADING = 0.25


def window_counts(line_count, column_count, first_column, strip_columns, half_lines, half_columns):
    line_index = jnp.arange(line_count, dtype=jnp.int32)
    column_index = first_column + jnp.arange(column_count, dtype=jnp.int32)
    line_span = (
        jnp.minimum(line_index + half_lines, line_count - 1)
        - jnp.maximum(line_index - half_lines, 0)
        + 1
    )
    column_span = (
        jnp.minimum(column_index + half_columns, strip_columns - 1)
        - jnp.maximum(column_index - half_columns, 0)
        + 1
    )
    return line_span.astype(jnp.float32)[:, None] * column_span.astype(jnp.float32)[None, :]


def box_window(products, column_count, half_lines, half_columns):
    summed = products[..., 0:column_count]
    for offset in range(1, 2 * half_columns + 1):
        summed = summed + products[..., offset : offset + column_count]
    line_count = summed.shape[-2]
    widths = [(0, 0)] * (summed.ndim - 2) + [(half_lines, half_lines), (0, 0)]
    padded = jnp.pad(summed, widths)
    result = padded[..., 0:line_count, :]
    for offset in range(1, 2 * half_lines + 1):
        result = result + padded[..., offset : offset + line_count, :]
    return result


def tile_covariance(window_data, counts, column_count):
    real_part = window_data[0]
    imag_part = window_data[1]

    def one_date(date_index):
        real_one = lax.dynamic_index_in_dim(real_part, date_index, 0, keepdims=True)
        imag_one = lax.dynamic_index_in_dim(imag_part, date_index, 0, keepdims=True)
        product_real = real_one * real_part + imag_one * imag_part
        product_imag = imag_one * real_part - real_one * imag_part
        stacked = jnp.stack([product_real, product_imag])
        return (box_window(stacked, column_count, HALF_Y, HALF_X) / counts).astype(jnp.bfloat16)

    return lax.map(one_date, jnp.arange(real_part.shape[0], dtype=jnp.int32))


def dct_table(line_count):
    frequency = jnp.arange(line_count, dtype=jnp.float32)[:, None]
    position = jnp.arange(line_count, dtype=jnp.float32)[None, :]
    weight = jnp.where(frequency == 0, math.sqrt(1.0 / line_count), math.sqrt(2.0 / line_count))
    return weight * jnp.cos(jnp.pi * (2.0 * position + 1.0) * frequency / (2.0 * line_count))


def link_tile(window_bf16, first_column, strip_columns, reference_date):
    window_data = window_bf16.astype(jnp.float32)
    column_count = window_data.shape[3] - 2 * HALF_X
    line_count = window_data.shape[2]
    counts = window_counts(line_count, column_count, first_column, strip_columns, HALF_Y, HALF_X)
    covariance = tile_covariance(window_data, counts, column_count)
    date_count = covariance.shape[0]
    pick = (jnp.arange(date_count, dtype=jnp.int32) == reference_date).astype(jnp.float32)[
        :, None, None
    ]
    start_real = jnp.broadcast_to(pick, (date_count, line_count, column_count))
    start_imag = jnp.zeros_like(start_real)

    def power_step(step_index, vector):
        vec_real, vec_imag = vector
        cov_real = covariance[:, 0].astype(jnp.float32)
        cov_imag = covariance[:, 1].astype(jnp.float32)
        new_real = (
            jnp.sum(cov_real * vec_real[None] - cov_imag * vec_imag[None], axis=1)
            + LOADING * vec_real
        )
        new_imag = (
            jnp.sum(cov_real * vec_imag[None] + cov_imag * vec_real[None], axis=1)
            + LOADING * vec_imag
        )
        length = jnp.sqrt(jnp.sum(new_real * new_real + new_imag * new_imag, axis=0))
        return (new_real / length, new_imag / length)

    vec_real, vec_imag = lax.fori_loop(0, POWER_ITERS, power_step, (start_real, start_imag))
    ref_real = jnp.sum(vec_real * pick, axis=0)
    ref_imag = jnp.sum(vec_imag * pick, axis=0)
    linked_real = DATES * (vec_real * ref_real + vec_imag * ref_imag)
    linked_imag = DATES * (vec_imag * ref_real - vec_real * ref_imag)
    center = window_data[..., HALF_X : HALF_X + column_count]
    scaling = 1.0 / math.sqrt(DATES)
    comp_real = jnp.sum(linked_real * center[0] + linked_imag * center[1], axis=0) * scaling
    comp_imag = jnp.sum(linked_real * center[1] - linked_imag * center[0], axis=0) * scaling
    return (linked_real, linked_imag, jnp.stack([comp_real, comp_imag]))


def transform_part(linked_part, table):
    date_count, line_count, column_count = linked_part.shape
    transformed = jnp.einsum("qr,krc->kqc", table, linked_part, precision=lax.Precision.HIGHEST)
    return transformed.reshape(date_count * line_count, column_count)


def on_device(slcs, ref_date):
    devices = lax.axis_size("pix")
    strip_columns = slcs.shape[2]
    column_count = strip_columns // devices
    local_rows = slcs.shape[1]
    first_column = lax.axis_index("pix") * column_count
    padded = jnp.pad(slcs, ((0, 0), (0, 0), (HALF_X, HALF_X)))
    left_rim = padded[:, :, 0:strip_columns].reshape(2, local_rows, devices, column_count)[
        ..., 0:HALF_X
    ]
    middle = padded[:, :, HALF_X : strip_columns + HALF_X].reshape(
        2, local_rows, devices, column_count
    )
    right_rim = padded[:, :, 2 * HALF_X : strip_columns + 2 * HALF_X].reshape(
        2, local_rows, devices, column_count
    )[..., column_count - HALF_X :]
    blocks = jnp.concatenate([left_rim, middle, right_rim], axis=3)
    blocks = blocks.reshape(2, local_rows, devices * (column_count + 2 * HALF_X))
    window_flat = lax.all_to_all(blocks, "pix", split_axis=2, concat_axis=1, tiled=True)
    window_bf16 = window_flat.reshape(2, DATES, ROWS, window_flat.shape[2])
    linked_real, linked_imag, compressed = link_tile(
        window_bf16, first_column, strip_columns, ref_date[0]
    )
    table = dct_table(ROWS)
    spectrum_tile = jnp.stack(
        [transform_part(linked_real, table), transform_part(linked_imag, table)]
    )
    spectrum = lax.all_to_all(spectrum_tile, "pix", split_axis=1, concat_axis=2, tiled=True)
    return (spectrum, compressed)


def solution(mesh):
    return jax.shard_map(
        on_device,
        mesh=mesh,
        in_specs=(P(None, ("grp", "pix"), None), P("grp")),
        out_specs=(P(None, ("grp", "pix"), None), P(None, None, ("grp", "pix"))),
        check_vma=False,
    )
```

profile of v0, /device:TPU:0, one launch (start us, length us, event | category | flops | bytes accessed | tf_op | source)
XLA Modules:
  0.0 232.7 jit_solution(5904203404528672844)
XLA Ops:
  0.6 1.6 pad_slice_fusion.25
  2.3 2.4 %copy.49 = bf16[2,64,2048]{1,0,2:T(2,128)(2,1)S(1)} copy(bf16[2,64,2048]{2,1,0:T(8,128)(2,1)} %param.6) | data formatting | bytes 1048576 | tf_op jit(solution)/shard_map/reshape | solution.py:125
  4.6 0.8 copy.48
  5.4 0.8 copy.50
  6.2 2.0 pad_maximum_fusion.1
  8.2 1.6 reshape.155
  9.8 7.4 %all-to-all-start = ((bf16[16,2,8832]{2,1,0:T(2,128)(2,1)}), bf16[16,2,8832]{2,1,0:T(2,128)(2,1)S(1)}, u32[]{:S(2)}, u32[]{:S(2)}) async-start(bf16[16,2,8832]{2,1,0:T(2,128)(2,1)} %reshape.155), calls=%async_computation | async-start | bytes 1130496 | tf_op jit(solution)/shard_map/all_to_all | solution.py:133
  17.9 14.2 %all-to-all-done = bf16[16,2,8832]{2,1,0:T(2,128)(2,1)S(1)} async-done(((bf16[16,2,8832]{2,1,0:T(2,128)(2,1)}), bf16[16,2,8832]{2,1,0:T(2,128)(2,1)S(1)}, u32[]{:S(2)}, u32[]{:S(2)}) %all-to-all-start) | async-done | bytes 565280 | tf_op jit(solution)/shard_map/all_to_all | solution.py:133
  32.1 0.7 reshape.156
  32.8 1.5 copy.36
  34.3 2.7 %reshape.149 = f32[2,64,16,138]{3,2,1,0:T(8,128)S(1)} reshape(bf16[2,64,2208]{2,1,0:T(8,128)(2,1)S(1)} %copy.36) | data formatting | bytes 1695744 | tf_op jit(solution)/shard_map/convert_element_type | solution.py:70
  37.3 1.2 copy-done
  38.5 0.6 copy.37
  39.1 0.6 copy.38
  39.7 124.0 %while.26 = (s32[]{:T(128)}, bf16[16,2,16,64,128]{4,3,2,1,0:T(8,128)(2,1)}, s32[16]{0:T(128)S(1)}, f32[16,64,138]{2,1,0:T(8,128)S(1)}, f32[16,64,138]{2,1,0:T(8,...) while((s32[]{:T(128)}, ...), condition=%wide.region_1.2_spmd.clone, body=%wide.region_0.1_spmd.clone.sunk | while | flops 7933957 | bytes 6291863 | solution.py:59
  39.8 0.6 dynamic_slice.28
  42.6 3.5 %fusion.59 = f32[2,16,64,128]{3,2,1,0:T(8,128)S(1)} fusion(f32[1,16,64,138]{3,2,1,0:T(8,128)S(1)} %get-tuple-element.277, f32[1,16,64,138]{3,2,1,0:T(8,128)S(1)} %get-tuple-element.278), kind=kLoop, calls=%fused_computation.32.clone.1 | loop fusion | flops 5505024 | bytes 2179072 | tf_op jit(solution)/shard_map/while/body/eval_jaxpr/add | solution.py:37
  46.2 1.3 bitcast_dynamic-update-slice_fusion.2
  50.3 3.5 %fusion.59 = f32[2,16,64,128]{3,2,1,0:T(8,128)S(1)} fusion(f32[1,16,64,138]{3,2,1,0:T(8,128)S(1)} %get-tuple-element.277, f32[1,16,64,138]{3,2,1,0:T(8,128)S(1)} %get-tuple-element.278), kind=kLoop, calls=%fused_computation.32.clone.1 | loop fusion | flops 5505024 | bytes 2179072 | tf_op jit(solution)/shard_map/while/body/eval_jaxpr/add | solution.py:37
  54.0 1.3 bitcast_dynamic-update-slice_fusion.2
  58.1 3.5 %fusion.59 = f32[2,16,64,128]{3,2,1,0:T(8,128)S(1)} fusion(f32[1,16,64,138]{3,2,1,0:T(8,128)S(1)} %get-tuple-element.277, f32[1,16,64,138]{3,2,1,0:T(8,128)S(1)} %get-tuple-element.278), kind=kLoop, calls=%fused_computation.32.clone.1 | loop fusion | flops 5505024 | bytes 2179072 | tf_op jit(solution)/shard_map/while/body/eval_jaxpr/add | solution.py:37
  61.7 1.3 bitcast_dynamic-update-slice_fusion.2
  65.9 3.5 %fusion.59 = f32[2,16,64,128]{3,2,1,0:T(8,128)S(1)} fusion(f32[1,16,64,138]{3,2,1,0:T(8,128)S(1)} %get-tuple-element.277, f32[1,16,64,138]{3,2,1,0:T(8,128)S(1)} %get-tuple-element.278), kind=kLoop, calls=%fused_computation.32.clone.1 | loop fusion | flops 5505024 | bytes 2179072 | tf_op jit(solution)/shard_map/while/body/eval_jaxpr/add | solution.py:37
  69.5 1.3 bitcast_dynamic-update-slice_fusion.2
  73.6 3.5 %fusion.59 = f32[2,16,64,128]{3,2,1,0:T(8,128)S(1)} fusion(f32[1,16,64,138]{3,2,1,0:T(8,128)S(1)} %get-tuple-element.277, f32[1,16,64,138]{3,2,1,0:T(8,128)S(1)} %get-tuple-element.278), kind=kLoop, calls=%fused_computation.32.clone.1 | loop fusion | flops 5505024 | bytes 2179072 | tf_op jit(solution)/shard_map/while/body/eval_jaxpr/add | solution.py:37
  77.2 1.3 bitcast_dynamic-update-slice_fusion.2
  81.4 3.5 %fusion.59 = f32[2,16,64,128]{3,2,1,0:T(8,128)S(1)} fusion(f32[1,16,64,138]{3,2,1,0:T(8,128)S(1)} %get-tuple-element.277, f32[1,16,64,138]{3,2,1,0:T(8,128)S(1)} %get-tuple-element.278), kind=kLoop, calls=%fused_computation.32.clone.1 | loop fusion | flops 5505024 | bytes 2179072 | tf_op jit(solution)/shard_map/while/body/eval_jaxpr/add | solution.py:37
  85.0 1.3 bitcast_dynamic-update-slice_fusion.2
  89.1 3.5 %fusion.59 = f32[2,16,64,128]{3,2,1,0:T(8,128)S(1)} fusion(f32[1,16,64,138]{3,2,1,0:T(8,128)S(1)} %get-tuple-element.277, f32[1,16,64,138]{3,2,1,0:T(8,128)S(1)} %get-tuple-element.278), kind=kLoop, calls=%fused_computation.32.clone.1 | loop fusion | flops 5505024 | bytes 2179072 | tf_op jit(solution)/shard_map/while/body/eval_jaxpr/add | solution.py:37
  92.7 1.3 bitcast_dynamic-update-slice_fusion.2
  96.8 3.5 %fusion.59 = f32[2,16,64,128]{3,2,1,0:T(8,128)S(1)} fusion(f32[1,16,64,138]{3,2,1,0:T(8,128)S(1)} %get-tuple-element.277, f32[1,16,64,138]{3,2,1,0:T(8,128)S(1)} %get-tuple-element.278), kind=kLoop, calls=%fused_computation.32.clone.1 | loop fusion | flops 5505024 | bytes 2179072 | tf_op jit(solution)/shard_map/while/body/eval_jaxpr/add | solution.py:37
  100.5 1.3 bitcast_dynamic-update-slice_fusion.2
  104.6 3.5 %fusion.59 = f32[2,16,64,128]{3,2,1,0:T(8,128)S(1)} fusion(f32[1,16,64,138]{3,2,1,0:T(8,128)S(1)} %get-tuple-element.277, f32[1,16,64,138]{3,2,1,0:T(8,128)S(1)} %get-tuple-element.278), kind=kLoop, calls=%fused_computation.32.clone.1 | loop fusion | flops 5505024 | bytes 2179072 | tf_op jit(solution)/shard_map/while/body/eval_jaxpr/add | solution.py:37
  108.2 1.3 bitcast_dynamic-update-slice_fusion.2
  112.3 3.5 %fusion.59 = f32[2,16,64,128]{3,2,1,0:T(8,128)S(1)} fusion(f32[1,16,64,138]{3,2,1,0:T(8,128)S(1)} %get-tuple-element.277, f32[1,16,64,138]{3,2,1,0:T(8,128)S(1)} %get-tuple-element.278), kind=kLoop, calls=%fused_computation.32.clone.1 | loop fusion | flops 5505024 | bytes 2179072 | tf_op jit(solution)/shard_map/while/body/eval_jaxpr/add | solution.py:37
  116.0 1.3 bitcast_dynamic-update-slice_fusion.2
  120.1 3.5 %fusion.59 = f32[2,16,64,128]{3,2,1,0:T(8,128)S(1)} fusion(f32[1,16,64,138]{3,2,1,0:T(8,128)S(1)} %get-tuple-element.277, f32[1,16,64,138]{3,2,1,0:T(8,128)S(1)} %get-tuple-element.278), kind=kLoop, calls=%fused_computation.32.clone.1 | loop fusion | flops 5505024 | bytes 2179072 | tf_op jit(solution)/shard_map/while/body/eval_jaxpr/add | solution.py:37
  123.7 1.3 bitcast_dynamic-update-slice_fusion.2
  127.9 3.5 %fusion.59 = f32[2,16,64,128]{3,2,1,0:T(8,128)S(1)} fusion(f32[1,16,64,138]{3,2,1,0:T(8,128)S(1)} %get-tuple-element.277, f32[1,16,64,138]{3,2,1,0:T(8,128)S(1)} %get-tuple-element.278), kind=kLoop, calls=%fused_computation.32.clone.1 | loop fusion | flops 5505024 | bytes 2179072 | tf_op jit(solution)/shard_map/while/body/eval_jaxpr/add | solution.py:37
  131.5 1.3 bitcast_dynamic-update-slice_fusion.2
  135.6 3.5 %fusion.59 = f32[2,16,64,128]{3,2,1,0:T(8,128)S(1)} fusion(f32[1,16,64,138]{3,2,1,0:T(8,128)S(1)} %get-tuple-element.277, f32[1,16,64,138]{3,2,1,0:T(8,128)S(1)} %get-tuple-element.278), kind=kLoop, calls=%fused_computation.32.clone.1 | loop fusion | flops 5505024 | bytes 2179072 | tf_op jit(solution)/shard_map/while/body/eval_jaxpr/add | solution.py:37
  139.2 1.3 bitcast_dynamic-update-slice_fusion.2
  143.4 3.5 %fusion.59 = f32[2,16,64,128]{3,2,1,0:T(8,128)S(1)} fusion(f32[1,16,64,138]{3,2,1,0:T(8,128)S(1)} %get-tuple-element.277, f32[1,16,64,138]{3,2,1,0:T(8,128)S(1)} %get-tuple-element.278), kind=kLoop, calls=%fused_computation.32.clone.1 | loop fusion | flops 5505024 | bytes 2179072 | tf_op jit(solution)/shard_map/while/body/eval_jaxpr/add | solution.py:37
  147.0 1.3 bitcast_dynamic-update-slice_fusion.2
  151.1 3.5 %fusion.59 = f32[2,16,64,128]{3,2,1,0:T(8,128)S(1)} fusion(f32[1,16,64,138]{3,2,1,0:T(8,128)S(1)} %get-tuple-element.277, f32[1,16,64,138]{3,2,1,0:T(8,128)S(1)} %get-tuple-element.278), kind=kLoop, calls=%fused_computation.32.clone.1 | loop fusion | flops 5505024 | bytes 2179072 | tf_op jit(solution)/shard_map/while/body/eval_jaxpr/add | solution.py:37
  154.8 1.3 bitcast_dynamic-update-slice_fusion.2
  158.9 3.5 %fusion.59 = f32[2,16,64,128]{3,2,1,0:T(8,128)S(1)} fusion(f32[1,16,64,138]{3,2,1,0:T(8,128)S(1)} %get-tuple-element.277, f32[1,16,64,138]{3,2,1,0:T(8,128)S(1)} %get-tuple-element.278), kind=kLoop, calls=%fused_computation.32.clone.1 | loop fusion | flops 5505024 | bytes 2179072 | tf_op jit(solution)/shard_map/while/body/eval_jaxpr/add | solution.py:37
  162.5 1.3 bitcast_dynamic-update-slice_fusion.2
  163.9 35.1 %while.27 = (s32[]{:T(128)}, f32[16,64,128]{2,1,0:T(8,128)S(1)}, f32[16,64,128]{2,1,0:T(8,128)S(1)}, bf16[16,2,16,64,128]{4,3,2,1,0:T(8,128)(2,1)}, s32[]{:T(128)}, /*index=5*/s32[]{:T(128)}) while((s32[]{:T(128)}, f32[16,64,128]{2,1,0:T(8,128)S(1)}, f32[16,64,128]{2,1,0:T(8,128)S(1)}, bf16[16,2,16,64,128]{4,3,2,1,0:T(8,128)(2,1)}, ...), condition=%wide.region_6.7_spmd.clone, body=%wide.region_2.6_spmd.clone.sunk | while | flops 22929412 | bytes 16908368 | solution.py:97
  164.0 5.3 %fusion.61 = (f32[16,64,128]{2,1,0:T(8,128)S(1)}, f32[16,64,128]{2,1,0:T(8,128)S(1)}) fusion(f32[16,64,128]{2,1,0:T(8,128)S(1)} %broadcast_select_fusion.2, f32[16,64,128]{2,1,0:T(8,128)S(1)} %get-tuple-element.324, bf16[16,2,16,64,128]{4,3,2,1,0:T(8,128)(2,1)} %get-tuple-element.332), kind=kLoop, calls=%fused_computation.69.clone.1 | loop fusion | flops 20709376 | bytes 10485760 | tf_op jit(solution)/shard_map/while/body/eval_jaxpr/reduce_sum | solution.py:91
  169.9 5.1 %fusion.61 = (f32[16,64,128]{2,1,0:T(8,128)S(1)}, f32[16,64,128]{2,1,0:T(8,128)S(1)}) fusion(f32[16,64,128]{2,1,0:T(8,128)S(1)} %broadcast_select_fusion.2, f32[16,64,128]{2,1,0:T(8,128)S(1)} %get-tuple-element.324, bf16[16,2,16,64,128]{4,3,2,1,0:T(8,128)(2,1)} %get-tuple-element.332), kind=kLoop, calls=%fused_computation.69.clone.1 | loop fusion | flops 20709376 | bytes 10485760 | tf_op jit(solution)/shard_map/while/body/eval_jaxpr/reduce_sum | solution.py:91
  175.7 5.1 %fusion.61 = (f32[16,64,128]{2,1,0:T(8,128)S(1)}, f32[16,64,128]{2,1,0:T(8,128)S(1)}) fusion(f32[16,64,128]{2,1,0:T(8,128)S(1)} %broadcast_select_fusion.2, f32[16,64,128]{2,1,0:T(8,128)S(1)} %get-tuple-element.324, bf16[16,2,16,64,128]{4,3,2,1,0:T(8,128)(2,1)} %get-tuple-element.332), kind=kLoop, calls=%fused_computation.69.clone.1 | loop fusion | flops 20709376 | bytes 10485760 | tf_op jit(solution)/shard_map/while/body/eval_jaxpr/reduce_sum | solution.py:91
  181.5 5.1 %fusion.61 = (f32[16,64,128]{2,1,0:T(8,128)S(1)}, f32[16,64,128]{2,1,0:T(8,128)S(1)}) fusion(f32[16,64,128]{2,1,0:T(8,128)S(1)} %broadcast_select_fusion.2, f32[16,64,128]{2,1,0:T(8,128)S(1)} %get-tuple-element.324, bf16[16,2,16,64,128]{4,3,2,1,0:T(8,128)(2,1)} %get-tuple-element.332), kind=kLoop, calls=%fused_computation.69.clone.1 | loop fusion | flops 20709376 | bytes 10485760 | tf_op jit(solution)/shard_map/while/body/eval_jaxpr/reduce_sum | solution.py:91
  187.3 5.1 %fusion.61 = (f32[16,64,128]{2,1,0:T(8,128)S(1)}, f32[16,64,128]{2,1,0:T(8,128)S(1)}) fusion(f32[16,64,128]{2,1,0:T(8,128)S(1)} %broadcast_select_fusion.2, f32[16,64,128]{2,1,0:T(8,128)S(1)} %get-tuple-element.324, bf16[16,2,16,64,128]{4,3,2,1,0:T(8,128)(2,1)} %get-tuple-element.332), kind=kLoop, calls=%fused_computation.69.clone.1 | loop fusion | flops 20709376 | bytes 10485760 | tf_op jit(solution)/shard_map/while/body/eval_jaxpr/reduce_sum | solution.py:91
  193.1 5.1 %fusion.61 = (f32[16,64,128]{2,1,0:T(8,128)S(1)}, f32[16,64,128]{2,1,0:T(8,128)S(1)}) fusion(f32[16,64,128]{2,1,0:T(8,128)S(1)} %broadcast_select_fusion.2, f32[16,64,128]{2,1,0:T(8,128)S(1)} %get-tuple-element.324, bf16[16,2,16,64,128]{4,3,2,1,0:T(8,128)(2,1)} %get-tuple-element.332), kind=kLoop, calls=%fused_computation.69.clone.1 | loop fusion | flops 20709376 | bytes 10485760 | tf_op jit(solution)/shard_map/while/body/eval_jaxpr/reduce_sum | solution.py:91
  199.2 0.9 add_reduce_fusion.1
  200.1 0.8 fusion.36
  200.9 0.8 fusion.34
  201.8 1.9 pad_maximum_fusion.2
  203.7 4.4 %all-to-all-start.1 = ((f32[2,1024,128]{2,0,1:T(2,128)}), f32[2,1024,128]{2,0,1:T(2,128)S(1)}, u32[]{:S(2)}, u32[]{:S(2)}) async-start(f32[2,1024,128]{2,0,1:T(2,128)} %pad_maximum_fusion.2), calls=%async_computation.1 | async-start | bytes 2097152 | tf_op jit(solution)/shard_map/all_to_all | solution.py:142
  208.1 0.6 pad_maximum_fusion.3
  208.7 22.2 %all-to-all-done.1 = f32[2,1024,128]{2,0,1:T(2,128)S(1)} async-done(((f32[2,1024,128]{2,0,1:T(2,128)}), f32[2,1024,128]{2,0,1:T(2,128)S(1)}, u32[]{:S(2)}, u32[]{:S(2)}) %all-to-all-start.1) | async-done | bytes 1048608 | tf_op jit(solution)/shard_map/all_to_all | solution.py:142
  230.9 0.6 copy.47
  231.5 1.1 all_to_all.24
  (103 shorter events, 18.9 us)
Async XLA Ops:
  9.8 22.4 %all-to-all-start = ((bf16[16,2,8832]{2,1,0:T(2,128)(2,1)}), bf16[16,2,8832]{2,1,0:T(2,128)(2,1)S(1)}, u32[]{:S(2)}, u32[]{:S(2)}) async-start(bf16[16,2,8832]{2,1,0:T(2,128)(2,1)} %reshape.155), calls=%async_computation | async-start | bytes 1130496 | tf_op jit(solution)/shard_map/all_to_all | solution.py:133
  37.1 1.4 copy-start
  163.9 35.3 %copy-start.1 = (f32[2,64,16,138]{3,2,1,0:T(8,128)S(1)}, f32[2,64,16,138]{3,2,1,0:T(8,128)}, u32[]{:S(2)}) copy-start(f32[2,64,16,138]{3,2,1,0:T(8,128)} %copy-done) | copy-start | bytes 3391492
  203.7 27.3 %all-to-all-start.1 = ((f32[2,1024,128]{2,0,1:T(2,128)}), f32[2,1024,128]{2,0,1:T(2,128)S(1)}, u32[]{:S(2)}, u32[]{:S(2)}) async-start(f32[2,1024,128]{2,0,1:T(2,128)} %pad_maximum_fusion.2), calls=%async_computation.1 | async-start | bytes 2097152 | tf_op jit(solution)/shard_map/all_to_all | solution.py:142
where the time goes:
time: 235 us; the launch traced here: 233 us
  other arithmetic  123 us (52%)
  waiting for transfers between devices  36.5 us (16%)
  loops' own time  32 us (14%)
  local copies, waits for them, and re-layouts  26.2 us (11%)
  starting transfers between devices  11.8 us (5%)
    add x16, other arithmetic, box_window(): summed = summed + products[..., offset:offset + column_count]  56.6 us
    another operation x1, loops' own time, tile_covariance(): return lax.map(one_date, jnp.arange(real_part.shape[0], dtype=jnp.int32))  31.5 us
    reduce_sum x6, other arithmetic, power_step(): jnp.sum(cov_real * vec_imag[None] + cov_imag * vec_real[None], axis=1)  31 us
    all_to_all x1, waiting for transfers between devices, on_device(): lax.all_to_all(spectrum_tile, 'pix', split_axis=1, concat_axis=2, tiled=T...  22.2 us
    dynamic_update_slice x16, other arithmetic, tile_covariance(): return lax.map(one_date, jnp.arange(real_part.shape[0], dtype=jnp.int32))  20.6 us
    all_to_all x1, waiting for transfers between devices, on_device(): lax.all_to_all(blocks, 'pix', split_axis=2, concat_axis=1, tiled=True)  14.2 us
    dynamic_slice x16, local copies, waits for them, and re-layouts, tile_covariance(): return lax.map(one_date, jnp.arange(real_part.shape[0], dtype=jnp.int32))  9.32 us
    all_to_all x1, starting transfers between devices, on_device(): lax.all_to_all(blocks, 'pix', split_axis=2, concat_axis=1, tiled=True)  7.41 us
  transfers between devices with their start and end apart: 2, of which 2 were waited for; matrix products, arithmetic and copies ran while one was open for 0% of the time, Pallas kernels for 0%

commit v1 on v0

v1 whole, which is shorter than its diff:
```python
import functools
import math

import jax
import jax.numpy as jnp
import numpy as np
from jax import lax
from jax.experimental import pallas as pl
from jax.experimental.pallas import tpu as pltpu
from jax.sharding import PartitionSpec as P

DATES = 16
ROWS = 64
HALF_X = 5
HALF_Y = 2
POWER_ITERS = 6
LOADING = 0.25

LANES = 128
SUB = 8
GROUPS = ROWS // SUB
HALO = LANES // GROUPS
REACH = DATES // 2
PLANES = 2 * (REACH + 1) - 1
MESH = pl.DeviceIdType.MESH


def line_order():
    return np.array([s * GROUPS + g for g in range(GROUPS) for s in range(SUB)])


def window_weights(columns):
    source = np.arange(columns)[:, None]
    target = np.arange(columns)[None, :]
    band = (np.abs(source - target) <= HALF_X).astype(np.float32)
    halo_column = np.concatenate([np.arange(-HALF_X, 0), columns + np.arange(HALF_X)])
    halo_band = np.zeros((HALO, columns), np.float32)
    halo_band[: 2 * HALF_X] = np.abs(halo_column[:, None] - target) <= HALF_X
    wide = np.zeros((GROUPS, HALO, GROUPS, columns), np.float32)
    for g in range(GROUPS):
        wide[g, :, g] = halo_band
    wide = wide.reshape(GROUPS * HALO, GROUPS // 2, 2 * columns).transpose(1, 0, 2)
    twice = np.concatenate([band, band], axis=0)
    wide_twice = np.concatenate([wide, wide], axis=1)
    return jnp.asarray(twice, jnp.bfloat16), jnp.asarray(wide_twice, jnp.bfloat16)


def dct_weights():
    frequency = np.arange(ROWS, dtype=np.float64)[:, None]
    position = np.arange(ROWS, dtype=np.float64)[None, :]
    weight = np.where(frequency == 0, math.sqrt(1.0 / ROWS), math.sqrt(2.0 / ROWS))
    table = weight * np.cos(np.pi * (2.0 * position + 1.0) * frequency / (2.0 * ROWS))
    table = table[:, line_order()].astype(np.float32)
    high = table.astype(jnp.bfloat16)
    low = (table - high.astype(np.float32)).astype(jnp.bfloat16)
    return jnp.asarray(np.concatenate([high, low, high], axis=1))


def greet(devices, me):
    barrier = pltpu.get_barrier_semaphore()
    for off in range(1, devices):
        pl.semaphore_signal(
            barrier, inc=1, device_id={"pix": lax.rem(me + off, devices)}, device_id_type=MESH
        )
    pl.semaphore_wait(barrier, devices - 1)


def gather_kernel(devices, x_ref, h_ref, w_ref, hw_ref, ssem, rsem, hs, hr, own):
    me = lax.axis_index("pix")
    columns = w_ref.shape[3]

    def block(d):
        return x_ref.at[:, :, pl.ds(pl.multiple_of(d * columns, columns), columns)]

    local = [
        pltpu.make_async_copy(block(me), w_ref.at[me], own.at[0]),
        pltpu.make_async_copy(h_ref.at[me], hw_ref.at[me], own.at[1]),
    ]
    for c in local:
        c.start()
    greet(devices, me)
    copies = []
    for off in range(1, devices):
        peer = lax.rem(me + off, devices)
        for src, dst, s, r in (
            (block(peer), w_ref.at[me], ssem, rsem),
            (h_ref.at[peer], hw_ref.at[me], hs, hr),
        ):
            c = pltpu.make_async_remote_copy(
                src_ref=src, dst_ref=dst, send_sem=s.at[off], recv_sem=r.at[off],
                device_id={"pix": peer}, device_id_type=MESH,
            )
            c.start()
            copies.append(c)
    for c in local + copies:
        c.wait()


def scatter_kernel(devices, t_ref, o_ref, ssem, rsem, own):
    me = lax.axis_index("pix")
    columns = t_ref.shape[3]
    mine = o_ref.at[:, :, pl.ds(pl.multiple_of(me * columns, columns), columns)]
    local = pltpu.make_async_copy(t_ref.at[me], mine, own)
    local.start()
    greet(devices, me)
    copies = [local]
    for off in range(1, devices):
        peer = lax.rem(me + off, devices)
        c = pltpu.make_async_remote_copy(
            src_ref=t_ref.at[peer], dst_ref=mine, send_sem=ssem.at[off], recv_sem=rsem.at[off],
            device_id={"pix": peer}, device_id_type=MESH,
        )
        c.start()
        copies.append(c)
    for c in copies:
        c.wait()


def split_halves(value):
    high = value.astype(jnp.bfloat16)
    low = (value - high.astype(jnp.float32)).astype(jnp.bfloat16)
    return high, low


def pair_products(read, i):
    real_one, imag_one = read(i, 0), read(i, 1)
    planes = [real_one * real_one + imag_one * imag_one]
    for d in range(1, REACH + 1):
        j = lax.rem(i + d, DATES)
        real_two, imag_two = read(j, 0), read(j, 1)
        planes.append(real_one * real_two + imag_one * imag_two)
        planes.append(imag_one * real_two - real_one * imag_two)
    return planes


def plane_of(d, part):
    return 0 if d == 0 else 2 * d - 1 + part


def link_kernel(strip_columns, ref_ref, w_ref, hw_ref, band_ref, wide_ref, dct_ref,
                spec_ref, comp_ref,
                stage, zf, hz, lhs_h, out_h, lhs, summed, inv, cov, vec, linked, comp):
    columns = w_ref.shape[3]
    first_column = lax.axis_index("pix") * columns
    sub = lax.broadcasted_iota(jnp.int32, (SUB, columns), 0)
    lane = lax.broadcasted_iota(jnp.int32, (SUB, columns), 1) + first_column
    across = jnp.minimum(lane + HALF_X, strip_columns - 1) - jnp.maximum(lane - HALF_X, 0) + 1
    for g in range(GROUPS):
        line = sub * GROUPS + g
        along = jnp.minimum(line + HALF_Y, ROWS - 1) - jnp.maximum(line - HALF_Y, 0) + 1
        inv[g] = 1.0 / (along * across).astype(jnp.float32)

    def prepare(k, carry):
        halo = hw_ref[k].astype(jnp.float32)
        for c in range(2):
            stage[c] = w_ref[k, c].astype(jnp.float32)
            hz[k, c] = halo[c * SUB:(c + 1) * SUB]
        for c in range(2):
            for g in range(GROUPS):
                zf[k, c, g] = stage[c, pl.ds(g, SUB, stride=GROUPS), :]
        return carry

    lax.fori_loop(0, DATES, prepare, 0)

    def halo_products(i, carry):
        planes = pair_products(lambda k, c: hz[k, c], i)
        planes.append(jnp.zeros_like(planes[0]))
        high, low = split_halves(jnp.concatenate(planes, axis=0))
        at = pl.ds(pl.multiple_of(i * (PLANES + 1) * SUB, 16), (PLANES + 1) * SUB)
        lhs_h[at, 0:LANES] = high
        lhs_h[at, LANES:2 * LANES] = low
        return carry

    lax.fori_loop(0, DATES, halo_products, 0)

    def halo_sums(n, carry):
        got = jnp.dot(lhs_h[...], wide_ref[n], preferred_element_type=jnp.float32)
        out_h[2 * n] = got[:, 0:columns]
        out_h[2 * n + 1] = got[:, columns:2 * columns]
        return carry

    lax.fori_loop(0, GROUPS // 2, halo_sums, 0)

    def covariances(i, carry):
        planes = pair_products(lambda k, c: zf[k, c].reshape(ROWS, columns), i)
        for p, value in enumerate(planes):
            high, low = split_halves(value)
            lhs[p * ROWS:(p + 1) * ROWS, 0:columns] = high
            lhs[p * ROWS:(p + 1) * ROWS, columns:2 * columns] = low
        summed[...] = jnp.dot(lhs[...], band_ref[...], preferred_element_type=jnp.float32)
        for d in range(REACH + 1):
            for part in range(1 if d == 0 else 2):
                p = plane_of(d, part)
                row = pl.multiple_of((i * (PLANES + 1) + p) * SUB, SUB)
                rows = [
                    summed[(p * GROUPS + g) * SUB:(p * GROUPS + g + 1) * SUB]
                    + out_h[g, pl.ds(row, SUB), :]
                    for g in range(GROUPS)
                ]
                before = [
                    jnp.where(sub == 0, 0.0, pltpu.roll(x, 1, 0)) for x in rows[-HALF_Y:]
                ]
                after = [
                    jnp.where(sub == SUB - 1, 0.0, pltpu.roll(x, SUB - 1, 0))
                    for x in rows[:HALF_Y]
                ]
                ext = before + rows + after
                two = [ext[q] + ext[q + 1] for q in range(GROUPS + 2)]
                for g in range(GROUPS):
                    value = (two[g] + two[g + 2] + ext[g + 4]) * inv[g]
                    if d == 0:
                        value = value + LOADING
                    cov[i, p, g] = value
        return carry

    lax.fori_loop(0, DATES, covariances, 0)

    ref = ref_ref[0]

    def solve(g, carry):
        for i in range(DATES):
            d = lax.rem(ref - i + DATES, DATES)
            fwd = d <= REACH
            dd = jnp.where(fwd, d, DATES - d)
            one = jnp.where(fwd, i, ref)
            pr = jnp.maximum(2 * dd - 1, 0)
            sign = jnp.where(d == 0, 0.0, jnp.where(fwd, 1.0, -1.0))
            vec[0, i, 0] = cov[one, pr, g]
            vec[0, i, 1] = cov[one, 2 * dd, g] * sign

        def step(t, carry):
            src = lax.rem(t, 2)
            for base in range(0, DATES, 8):
                real = [None] * 8
                imag = [None] * 8
                for j in range(DATES):
                    vr, vi = vec[src, j, 0], vec[src, j, 1]
                    for q in range(8):
                        i = base + q
                        d = (j - i) % DATES
                        if d == 0:
                            cr = cov[i, 0, g]
                            add_r, add_i = cr * vr, cr * vi
                        elif d <= REACH:
                            cr, ci = cov[i, 2 * d - 1, g], cov[i, 2 * d, g]
                            add_r, add_i = cr * vr - ci * vi, cr * vi + ci * vr
                        else:
                            d = DATES - d
                            cr, ci = cov[j, 2 * d - 1, g], cov[j, 2 * d, g]
                            add_r, add_i = cr * vr + ci * vi, cr * vi - ci * vr
                        real[q] = add_r if real[q] is None else real[q] + add_r
                        imag[q] = add_i if imag[q] is None else imag[q] + add_i
                for q in range(8):
                    vec[1 - src, base + q, 0] = real[q]
                    vec[1 - src, base + q, 1] = imag[q]
            return carry

        lax.fori_loop(0, POWER_ITERS - 1, step, 0)
        last = (POWER_ITERS - 1) % 2
        total = jnp.zeros((SUB, columns), jnp.float32)
        for k in range(DATES):
            vr, vi = vec[last, k, 0], vec[last, k, 1]
            total = total + (vr * vr + vi * vi)
        scale = DATES / total
        rr, ri = vec[last, ref, 0] * scale, vec[last, ref, 1] * scale
        comp_r = jnp.zeros_like(total)
        comp_i = jnp.zeros_like(total)
        at = pl.ds(pl.multiple_of(g * SUB, SUB), SUB)
        for k in range(DATES):
            vr, vi = vec[last, k, 0], vec[last, k, 1]
            lr = vr * rr + vi * ri
            li = vi * rr - vr * ri
            zr, zi = zf[k, 0, g], zf[k, 1, g]
            comp_r = comp_r + (lr * zr + li * zi)
            comp_i = comp_i + (lr * zi - li * zr)
            linked[k, at, 0:columns] = lr
            linked[k, at, columns:2 * columns] = li
        comp[0, g] = comp_r * (1.0 / math.sqrt(DATES))
        comp[1, g] = comp_i * (1.0 / math.sqrt(DATES))
        return carry

    lax.fori_loop(0, GROUPS, solve, 0)
    for c in range(2):
        for g in range(GROUPS):
            comp_ref[c, pl.ds(g, SUB, stride=GROUPS), :] = comp[c, g]

    def transform(k, carry):
        high, low = split_halves(linked[k])
        both = jnp.concatenate([high, high, low], axis=0)
        got = jnp.dot(dct_ref[...], both, preferred_element_type=jnp.float32)
        got = got.astype(spec_ref.dtype)
        spec_ref[k, 0] = got[:, 0:columns]
        spec_ref[k, 1] = got[:, columns:2 * columns]
        return carry

    lax.fori_loop(0, DATES, transform, 0)


def link_call(strip_columns, ref_date, window, halo):
    columns = window.shape[3]
    band, wide = window_weights(columns)
    f32, bf16 = jnp.float32, jnp.bfloat16
    vmem = pl.BlockSpec(memory_space=pltpu.VMEM)
    return pl.pallas_call(
        functools.partial(link_kernel, strip_columns),
        out_shape=(
            jax.ShapeDtypeStruct((DATES, 2, ROWS, columns), bf16),
            jax.ShapeDtypeStruct((2, ROWS, columns), f32),
        ),
        in_specs=[pl.BlockSpec(memory_space=pltpu.SMEM)] + [vmem] * 5,
        out_specs=(vmem, vmem),
        scratch_shapes=[
            pltpu.VMEM((2, ROWS, columns), f32),
            pltpu.VMEM((DATES, 2, GROUPS, SUB, columns), f32),
            pltpu.VMEM((DATES, 2, SUB, LANES), f32),
            pltpu.VMEM((DATES * (PLANES + 1) * SUB, 2 * LANES), bf16),
            pltpu.VMEM((GROUPS, DATES * (PLANES + 1) * SUB, columns), f32),
            pltpu.VMEM((PLANES * ROWS, 2 * columns), bf16),
            pltpu.VMEM((PLANES * ROWS, columns), f32),
            pltpu.VMEM((GROUPS, SUB, columns), f32),
            pltpu.VMEM((DATES, PLANES, GROUPS, SUB, columns), f32),
            pltpu.VMEM((2, DATES, 2, SUB, columns), f32),
            pltpu.VMEM((DATES, ROWS, 2 * columns), f32),
            pltpu.VMEM((2, GROUPS, SUB, columns), f32),
        ],
        compiler_params=pltpu.CompilerParams(vmem_limit_bytes=56 * 1024 * 1024),
        name="link",
    )(ref_date, window, halo, band, wide, dct_weights())


def on_device(slcs, ref_date):
    devices = lax.axis_size("pix")
    local_rows, strip_columns = slcs.shape[1], slcs.shape[2]
    columns = strip_columns // devices
    per_date = ROWS // local_rows
    lines = local_rows // GROUPS
    pad_rows = max(16, 2 * lines)

    cut = slcs.reshape(2, local_rows, devices, columns)
    edge = jnp.zeros((2, local_rows, 1, HALF_X), slcs.dtype)
    left = jnp.concatenate([edge, cut[:, :, :-1, columns - HALF_X:]], axis=2)
    right = jnp.concatenate([cut[:, :, 1:, :HALF_X], edge], axis=2)
    fill = jnp.zeros((2, local_rows, devices, HALO - 2 * HALF_X), slcs.dtype)
    halo = jnp.concatenate([left, right, fill], axis=3)
    halo = halo.reshape(2, lines, GROUPS, devices, HALO).transpose(3, 0, 1, 2, 4)
    halo = halo.reshape(devices, 2 * lines, LANES)
    halo = jnp.pad(halo, ((0, 0), (0, pad_rows - 2 * lines), (0, 0)))

    anywhere = pl.BlockSpec(memory_space=pl.ANY)
    sems = pltpu.SemaphoreType.DMA((devices,))
    window, halo = pl.pallas_call(
        functools.partial(gather_kernel, devices),
        out_shape=(
            jax.ShapeDtypeStruct((devices, 2, local_rows, columns), slcs.dtype),
            jax.ShapeDtypeStruct(halo.shape, slcs.dtype),
        ),
        in_specs=[anywhere] * 2,
        out_specs=(anywhere, anywhere),
        scratch_shapes=[sems] * 4 + [pltpu.SemaphoreType.DMA((2,))],
        compiler_params=pltpu.CompilerParams(collective_id=0, has_side_effects=True),
        name="gather",
    )(slcs, halo)

    if per_date > 1:
        window = window.reshape(DATES, per_date, 2, local_rows, columns).transpose(0, 2, 1, 3, 4)
        halo = halo[:, :2 * lines].reshape(DATES, per_date, 2, lines, LANES)
        halo = halo.transpose(0, 2, 1, 3, 4)
    window = window.reshape(DATES, 2, ROWS, columns)
    halo = halo.reshape(DATES, 2 * SUB, LANES)

    tile, compressed = link_call(strip_columns, ref_date, window, halo)

    if per_date > 1:
        tile = tile.reshape(DATES, 2, per_date, local_rows, columns).transpose(0, 2, 1, 3, 4)
    tile = tile.reshape(devices, 2, local_rows, columns)
    spectrum = pl.pallas_call(
        functools.partial(scatter_kernel, devices),
        out_shape=jax.ShapeDtypeStruct((2, local_rows, strip_columns), tile.dtype),
        in_specs=[anywhere],
        out_specs=anywhere,
        scratch_shapes=[sems] * 2 + [pltpu.SemaphoreType.DMA],
        compiler_params=pltpu.CompilerParams(collective_id=1, has_side_effects=True),
        name="scatter",
    )(tile)
    return (spectrum.astype(jnp.float32), compressed)


def solution(mesh):
    return jax.shard_map(
        on_device,
        mesh=mesh,
        in_specs=(P(None, ("grp", "pix"), None), P("grp")),
        out_specs=(P(None, ("grp", "pix"), None), P(None, None, ("grp", "pix"))),
        check_vma=False,
    )
```

time: 235 us -> 66.3 us (0.28)
  the two profiles are of different devices: /device:TPU:0 before, /device:TPU:15 now
where the time goes in v1:
time: 66.3 us; the launch traced here: 66.1 us
  Pallas kernels  59.7 us (90%)
  local copies, waits for them, and re-layouts  2.87 us (4%)
  other arithmetic  2.22 us (3%)
  between operations  1.33 us (2%)
    pallas_call x1, Pallas kernels, link_call(): pl.pallas_call(functools.partial(link_kernel, strip_columns), out_shape=(...  24.8 us
    pallas_call x1, Pallas kernels, on_device(): pl.pallas_call(functools.partial(gather_kernel, devices), out_shape=(jax....  18.6 us
    pallas_call x1, Pallas kernels, on_device(): pl.pallas_call(functools.partial(scatter_kernel, devices), out_shape=jax....  16.3 us
    convert_element_type x1, other arithmetic, on_device(): return (spectrum.astype(jnp.float32), compressed)  2.12 us
    unnamed x1, local copies, waits for them, and re-layouts  1.51 us

profile of v1, /device:TPU:15, one launch (start us, length us, event | category | flops | bytes accessed | tf_op | source)
XLA Modules:
  0.0 66.1 jit_solution(12484444859182999815)
XLA Ops:
  1.3 0.1 pad.4.clone
  1.4 1.5 %copy.11 = bf16[2,64,2048]{1,2,0:T(8,128)(2,1)S(1)} copy(bf16[2,64,2048]{2,1,0:T(8,128)(2,1)} %x_ref.1) | data formatting | bytes 1048576 | tf_op args[0]
  2.9 0.1 fusion.4
  3.0 0.3 copy.14
  3.3 1.0 %reshape.15.h_ref = bf16[16,16,128]{2,1,0:T(8,128)(2,1)} reshape(bf16[16,2,8,8,16]{4,3,2,1,0:T(8,128)(2,1)S(1)} %bitcast.6) | data formatting | bytes 131072 | tf_op jit(solution)/shard_map/reshape | solution.py:346
  4.3 18.6 %gather.1 = (bf16[16,2,64,128]{3,2,1,0:T(8,128)(2,1)}, bf16[16,16,128]{2,1,0:T(8,128)(2,1)}) custom-call(bf16[2,64,2048]{2,1,0:T(8,128)(2,1)} %x_ref.1, bf16[16,16,128]{2,1,0:T(8,128)(2,1)} %reshape.15.h_ref), custom_call_target="tpu_custom_call" | custom-call | tf_op jit(solution)/shard_map/gather/pallas_call | solution.py:351
  22.9 24.8 %link.1 = (bf16[16,2,64,128]{3,2,1,0:T(8,128)(2,1)}, f32[2,64,128]{2,1,0:T(8,128)}) custom-call(s32[1]{0:T(128)S(6)} %copy.15.ref_ref, bf16[16,2,64,128]{3,2,1,0:T(8,128)(2,1)} %get-tuple-element.6.w_ref, bf16[16,16,128]{2,1,0:T(8,128)(2,1)} %get-tuple-element.7.hw_ref, bf16[256,128]{1,0:T(8,128)(2,1)} %constant.5.clone.band_ref, ...), custom_call_target="tpu_custom_call" | custom-call | tf_op jit(solution)/shard_map/link/pallas_call | solution.py:304
  47.6 16.3 %scatter.1 = bf16[2,64,2048]{2,1,0:T(8,128)(2,1)} custom-call(bf16[16,2,64,128]{3,2,1,0:T(8,128)(2,1)} %get-tuple-element.8.t_ref), custom_call_target="tpu_custom_call" | custom-call | tf_op jit(solution)/shard_map/scatter/pallas_call | solution.py:376
  63.9 2.1 %convert_element_type.3 = f32[2,64,2048]{2,1,0:T(8,128)} convert(bf16[2,64,2048]{2,1,0:T(8,128)(2,1)} %scatter.1) | non-fusion elementwise | flops 262144 | bytes 1572864 | tf_op jit(solution)/shard_map/convert_element_type | solution.py:385
  (2 shorter events, 0.0 us)

commit v2 on v1

v2 whole, which is shorter than its diff:
```python
import functools
import math

import jax
import jax.numpy as jnp
import numpy as np
from jax import lax
from jax.experimental import pallas as pl
from jax.experimental.pallas import tpu as pltpu
from jax.sharding import PartitionSpec as P

DATES = 16
ROWS = 64
HALF_X = 5
HALF_Y = 2
POWER_ITERS = 6
LOADING = 0.25

LANES = 128
SUB = 8
GROUPS = ROWS // SUB
HALO = LANES // GROUPS
CHUNK = 4
SPAN = 8
MESH = pl.DeviceIdType.MESH


def line_order():
    return np.array([s * GROUPS + g for g in range(GROUPS) for s in range(SUB)])


def window_weights(columns):
    source = np.arange(columns)[:, None]
    target = np.arange(columns)[None, :]
    band = (np.abs(source - target) <= HALF_X).astype(np.float32)
    halo_column = np.concatenate([np.arange(-HALF_X, 0), columns + np.arange(HALF_X)])
    halo_band = np.zeros((HALO, columns), np.float32)
    halo_band[: 2 * HALF_X] = np.abs(halo_column[:, None] - target) <= HALF_X
    wide = np.zeros((GROUPS, HALO, GROUPS, columns), np.float32)
    for g in range(GROUPS):
        wide[g, :, g] = halo_band
    wide = wide.reshape(GROUPS * HALO, GROUPS // 2, 2 * columns).transpose(1, 0, 2)
    twice = np.concatenate([band, band], axis=0)
    wide_twice = np.concatenate([wide, wide], axis=1)
    return jnp.asarray(twice, jnp.bfloat16), jnp.asarray(wide_twice, jnp.bfloat16)


def dct_weights():
    frequency = np.arange(ROWS, dtype=np.float64)[:, None]
    position = np.arange(ROWS, dtype=np.float64)[None, :]
    weight = np.where(frequency == 0, math.sqrt(1.0 / ROWS), math.sqrt(2.0 / ROWS))
    table = weight * np.cos(np.pi * (2.0 * position + 1.0) * frequency / (2.0 * ROWS))
    table = table[:, line_order()].astype(np.float32)
    high = table.astype(jnp.bfloat16)
    low = (table - high.astype(np.float32)).astype(jnp.bfloat16)
    return jnp.asarray(np.concatenate([high, low, high], axis=1))


def split_halves(value):
    high = value.astype(jnp.bfloat16)
    low = (value - high.astype(jnp.float32)).astype(jnp.bfloat16)
    return high, low


def pair_products(one, two):
    real = one[0] * two[0] + one[1] * two[1]
    imag = one[1] * two[0] - one[0] * two[1]
    return real, imag


def chunk_index(p):
    whole, rest = p // CHUNK, p % CHUNK
    return (whole + 1) * (whole * (CHUNK // 2) + rest)


def link_kernel(devices, ref_ref, h_ref, x_ref, band_ref, wide_ref, dct_ref,
                o_ref, comp_ref,
                xs, win, hwin, band, wide, dct, stage, zf, hz, lhs_h, out_h, lhs, summed, inv,
                cov, vec, linked, comp, tile,
                local, ssem, rsem, hs, hr, ts, tr):
    columns = win.shape[3]
    local_rows = win.shape[2]
    strip_columns = x_ref.shape[2]
    per_date = ROWS // local_rows
    lines = local_rows // GROUPS
    me = lax.axis_index("pix")
    my_date = me // per_date

    loads = [
        pltpu.make_async_copy(src, dst, local.at[n])
        for n, (src, dst) in enumerate(
            ((x_ref, xs), (wide_ref, wide), (band_ref, band), (dct_ref, dct))
        )
    ]
    for load in loads:
        load.start()
    barrier = pltpu.get_barrier_semaphore()
    for off in range(1, devices):
        pl.semaphore_signal(
            barrier, inc=1, device_id={"pix": lax.rem(me + off, devices)}, device_id_type=MESH
        )

    first_column = me * columns
    sub = lax.broadcasted_iota(jnp.int32, (SUB, columns), 0)
    lane = lax.broadcasted_iota(jnp.int32, (SUB, columns), 1) + first_column
    across = jnp.minimum(lane + HALF_X, strip_columns - 1) - jnp.maximum(lane - HALF_X, 0) + 1
    for g in range(GROUPS):
        line = sub * GROUPS + g
        along = jnp.minimum(line + HALF_Y, ROWS - 1) - jnp.maximum(line - HALF_Y, 0) + 1
        inv[g] = 1.0 / (along * across).astype(jnp.float32)

    pl.semaphore_wait(barrier, devices - 1)
    loads[0].wait()

    def block(n):
        return xs.at[:, :, pl.ds(pl.multiple_of(n * columns, columns), columns)]

    def main_copy(off):
        peer = lax.rem(me + off, devices)
        return pltpu.make_async_remote_copy(
            src_ref=block(peer), dst_ref=win.at[me], send_sem=ssem.at[off], recv_sem=rsem.at[off],
            device_id={"pix": peer}, device_id_type=MESH,
        )

    def halo_copy(off):
        peer = lax.rem(me + off, devices)
        return pltpu.make_async_remote_copy(
            src_ref=h_ref.at[peer], dst_ref=hwin.at[me], send_sem=hs.at[off],
            recv_sem=hr.at[off], device_id={"pix": peer}, device_id_type=MESH,
        )

    halos = [halo_copy(off) for off in range(1, devices)]
    mains = [main_copy(off) for off in range(1, devices)]
    for c in halos + mains:
        c.start()
    own = [
        pltpu.make_async_copy(block(me), win.at[me], local.at[4]),
        pltpu.make_async_copy(h_ref.at[me], hwin.at[me], local.at[5]),
    ]
    for c in own:
        c.start()
    for c in own + loads[1:] + halos:
        c.wait()

    def date_at(p):
        return lax.rem(my_date - p + DATES, DATES)

    def prepare_halo(p, carry):
        for q in range(per_date):
            halo = hwin[date_at(p) * per_date + q].astype(jnp.float32)
            for c in range(2):
                hz[p, c, q * lines:(q + 1) * lines] = halo[c * lines:(c + 1) * lines]
        return carry

    lax.fori_loop(0, DATES, prepare_halo, 0)

    def halo_products(p, carry):
        one = hz[p, 0], hz[p, 1]

        def chunk(n, carry):
            planes = []
            for q in range(CHUNK):
                planes += pair_products(one, (hz[n * CHUNK + q, 0], hz[n * CHUNK + q, 1]))
            high, low = split_halves(jnp.concatenate(planes, axis=0))
            size = 2 * CHUNK * SUB
            at = pl.ds(pl.multiple_of((chunk_index(p) + n) * size, size), size)
            lhs_h[at, 0:LANES] = high
            lhs_h[at, LANES:2 * LANES] = low
            return carry

        return lax.fori_loop(0, p // CHUNK + 1, chunk, carry)

    lax.fori_loop(0, DATES, halo_products, 0)

    def halo_sums(n, carry):
        got = jnp.dot(lhs_h[...], wide[n], preferred_element_type=jnp.float32)
        out_h[2 * n] = got[:, 0:columns]
        out_h[2 * n + 1] = got[:, columns:2 * columns]
        return carry

    lax.fori_loop(0, GROUPS // 2, halo_sums, 0)

    def window_sums(row, first):
        rows = [
            summed[first + g * SUB:first + (g + 1) * SUB] + out_h[g, pl.ds(row, SUB), :]
            for g in range(GROUPS)
        ]
        before = [jnp.where(sub == 0, 0.0, pltpu.roll(x, 1, 0)) for x in rows[-HALF_Y:]]
        after = [jnp.where(sub == SUB - 1, 0.0, pltpu.roll(x, SUB - 1, 0)) for x in rows[:HALF_Y]]
        ext = before + rows + after
        two = [ext[g] + ext[g + 1] for g in range(GROUPS + 2)]
        return [(two[g] + two[g + 2] + ext[g + 4]) * inv[g] for g in range(GROUPS)]

    def covariances(p, carry):
        for q in range(per_date):
            source = date_at(p) * per_date + q
            off = lax.rem(me - source + devices, devices)

            @pl.when(off != 0)
            def _():
                main_copy(off).wait_recv()

            for c in range(2):
                stage[c, q * local_rows:(q + 1) * local_rows] = win[source, c].astype(jnp.float32)
        for c in range(2):
            for g in range(GROUPS):
                zf[p, c, g] = stage[c, pl.ds(g, SUB, stride=GROUPS), :]

        def chunk(n, carry):
            one = zf[p, 0].reshape(ROWS, columns), zf[p, 1].reshape(ROWS, columns)
            for q in range(CHUNK):
                k = n * CHUNK + q
                two = zf[k, 0].reshape(ROWS, columns), zf[k, 1].reshape(ROWS, columns)
                for part, value in enumerate(pair_products(one, two)):
                    high, low = split_halves(value)
                    at = (2 * q + part) * ROWS
                    lhs[at:at + ROWS, 0:columns] = high
                    lhs[at:at + ROWS, columns:2 * columns] = low
            summed[...] = jnp.dot(lhs[...], band[...], preferred_element_type=jnp.float32)
            size = 2 * CHUNK * SUB
            base = (chunk_index(p) + n) * size
            for q in range(CHUNK):
                sums = [
                    window_sums(
                        pl.multiple_of(base + (2 * q + part) * SUB, SUB), (2 * q + part) * ROWS
                    )
                    for part in range(2)
                ]
                for g in range(GROUPS):
                    real, imag = sums[0][g], sums[1][g]
                    cov[p, n * CHUNK + q, 0, g] = real
                    cov[p, n * CHUNK + q, 1, g] = real + imag
                    cov[p, n * CHUNK + q, 2, g] = imag - real
            return carry

        lax.fori_loop(0, p // CHUNK + 1, chunk, 0)
        for g in range(GROUPS):
            cov[p, p, 0, g] = cov[p, p, 0, g] + LOADING
        return carry

    lax.fori_loop(0, DATES, covariances, 0)

    ref = lax.rem(my_date - ref_ref[0] + DATES, DATES)

    def solve(g, carry):
        for i in range(DATES):
            one, two = jnp.maximum(ref, i), jnp.minimum(ref, i)
            real = cov[one, two, 0, g]
            imag = 0.5 * (cov[one, two, 1, g] + cov[one, two, 2, g])
            sign = jnp.where(ref == i, 0.0, jnp.where(ref < i, 1.0, -1.0))
            imag = imag * sign
            vec[0, i, 0] = real
            vec[0, i, 1] = imag
            vec[0, i, 2] = real + imag

        def step(t, carry):
            src = lax.rem(t, 2)
            for base in range(0, DATES, SPAN):
                acc = [[None] * 3 for _ in range(SPAN)]
                for j in range(DATES):
                    vr, vi, vs = vec[src, j, 0], vec[src, j, 1], vec[src, j, 2]
                    for q in range(SPAN):
                        i = base + q
                        one, two = max(i, j), min(i, j)
                        cr = cov[one, two, 0, g]
                        if i == j:
                            terms = (cr * vs, cr * vi, -(cr * vr))
                        elif i > j:
                            terms = (cr * vs, cov[i, j, 1, g] * vi, cov[i, j, 2, g] * vr)
                        else:
                            terms = (cr * vs, -(cov[j, i, 2, g] * vi), -(cov[j, i, 1, g] * vr))
                        for n in range(3):
                            acc[q][n] = terms[n] if acc[q][n] is None else acc[q][n] + terms[n]
                for q in range(SPAN):
                    real, imag = acc[q][0] - acc[q][1], acc[q][0] + acc[q][2]
                    vec[1 - src, base + q, 0] = real
                    vec[1 - src, base + q, 1] = imag
                    vec[1 - src, base + q, 2] = real + imag
            return carry

        lax.fori_loop(0, POWER_ITERS - 1, step, 0)
        last = (POWER_ITERS - 1) % 2
        total = jnp.zeros((SUB, columns), jnp.float32)
        for k in range(DATES):
            vr, vi = vec[last, k, 0], vec[last, k, 1]
            total = total + (vr * vr + vi * vi)
        scale = DATES / total
        rr, ri = vec[last, ref, 0] * scale, vec[last, ref, 1] * scale
        comp_r = jnp.zeros_like(total)
        comp_i = jnp.zeros_like(total)
        at = pl.ds(pl.multiple_of(g * SUB, SUB), SUB)
        for k in range(DATES):
            vr, vi = vec[last, k, 0], vec[last, k, 1]
            lr = vr * rr + vi * ri
            li = vi * rr - vr * ri
            zr, zi = zf[k, 0, g], zf[k, 1, g]
            comp_r = comp_r + (lr * zr + li * zi)
            comp_i = comp_i + (lr * zi - li * zr)
            linked[k, at, 0:columns] = lr
            linked[k, at, columns:2 * columns] = li
        comp[0, g] = comp_r * (1.0 / math.sqrt(DATES))
        comp[1, g] = comp_i * (1.0 / math.sqrt(DATES))
        return carry

    lax.fori_loop(0, GROUPS, solve, 0)

    mine = o_ref.at[:, :, pl.ds(pl.multiple_of(first_column, columns), columns)]

    def tile_copy(p, q):
        peer = date_at(p) * per_date + q
        off = lax.rem(peer - me + devices, devices)
        return off, pltpu.make_async_remote_copy(
            src_ref=tile.at[p, :, q * local_rows:(q + 1) * local_rows, :], dst_ref=mine,
            send_sem=ts.at[off], recv_sem=tr.at[off],
            device_id={"pix": peer}, device_id_type=MESH,
        )

    def send(p):
        for q in range(per_date):
            off, copy = tile_copy(p, q)

            @pl.when(off != 0)
            def _():
                copy.start()

            @pl.when(off == 0)
            def _():
                pltpu.make_async_copy(
                    tile.at[p, :, q * local_rows:(q + 1) * local_rows, :], mine, local.at[6]
                ).start()

    def transform(p, carry):
        high, low = split_halves(linked[p])
        both = jnp.concatenate([high, high, low], axis=0)
        got = jnp.dot(dct[...], both, preferred_element_type=jnp.float32).astype(tile.dtype)
        tile[p, 0] = got[:, 0:columns]
        tile[p, 1] = got[:, columns:2 * columns]

        @pl.when(p > 0)
        def _():
            send(p - 1)

        return carry

    lax.fori_loop(0, DATES, transform, 0)
    for c in range(2):
        for g in range(GROUPS):
            comp_ref[c, pl.ds(g, SUB, stride=GROUPS), :] = comp[c, g]
    send(DATES - 1)

    for c in mains:
        c.wait_send()
    own_tile = tile.at[0, :, 0:local_rows, :]
    pltpu.make_async_copy(own_tile, mine, local.at[6]).wait()
    for off in range(1, devices):
        pltpu.make_async_remote_copy(
            src_ref=own_tile, dst_ref=mine, send_sem=ts.at[off], recv_sem=tr.at[off],
            device_id={"pix": lax.rem(me + off, devices)}, device_id_type=MESH,
        ).wait()


def on_device(slcs, ref_date):
    devices = lax.axis_size("pix")
    local_rows, strip_columns = slcs.shape[1], slcs.shape[2]
    columns = strip_columns // devices
    per_date = ROWS // local_rows
    lines = local_rows // GROUPS
    pad_rows = max(16, 2 * lines)

    cut = slcs.reshape(2, local_rows, devices, columns)
    edge = jnp.zeros((2, local_rows, 1, HALF_X), slcs.dtype)
    left = jnp.concatenate([edge, cut[:, :, :-1, columns - HALF_X:]], axis=2)
    right = jnp.concatenate([cut[:, :, 1:, :HALF_X], edge], axis=2)
    fill = jnp.zeros((2, local_rows, devices, HALO - 2 * HALF_X), slcs.dtype)
    halo = jnp.concatenate([left, right, fill], axis=3)
    halo = halo.reshape(2, lines, GROUPS, devices, HALO).transpose(3, 0, 1, 2, 4)
    halo = halo.reshape(devices, 2 * lines, LANES)
    halo = jnp.pad(halo, ((0, 0), (0, pad_rows - 2 * lines), (0, 0)))

    anywhere = pl.BlockSpec(memory_space=pl.ANY)
    vmem = pl.BlockSpec(memory_space=pltpu.VMEM)
    band, wide = window_weights(columns)
    dct = dct_weights()
    f32, bf16 = jnp.float32, jnp.bfloat16
    halo_lines = chunk_index(DATES) * 2 * CHUNK * SUB
    sems = pltpu.SemaphoreType.DMA((devices,))
    spectrum, compressed = pl.pallas_call(
        functools.partial(link_kernel, devices),
        out_shape=(
            jax.ShapeDtypeStruct((2, local_rows, strip_columns), bf16),
            jax.ShapeDtypeStruct((2, ROWS, columns), f32),
        ),
        in_specs=[pl.BlockSpec(memory_space=pltpu.SMEM), vmem] + [anywhere] * 4,
        out_specs=(anywhere, vmem),
        scratch_shapes=[
            pltpu.VMEM(slcs.shape, bf16),
            pltpu.VMEM((devices, 2, local_rows, columns), bf16),
            pltpu.VMEM(halo.shape, bf16),
            pltpu.VMEM(band.shape, bf16),
            pltpu.VMEM(wide.shape, bf16),
            pltpu.VMEM(dct.shape, bf16),
            pltpu.VMEM((2, ROWS, columns), f32),
            pltpu.VMEM((DATES, 2, GROUPS, SUB, columns), f32),
            pltpu.VMEM((DATES, 2, SUB, LANES), f32),
            pltpu.VMEM((halo_lines, 2 * LANES), bf16),
            pltpu.VMEM((GROUPS, halo_lines, columns), f32),
            pltpu.VMEM((2 * CHUNK * ROWS, 2 * columns), bf16),
            pltpu.VMEM((2 * CHUNK * ROWS, columns), f32),
            pltpu.VMEM((GROUPS, SUB, columns), f32),
            pltpu.VMEM((DATES, DATES, 3, GROUPS, SUB, columns), f32),
            pltpu.VMEM((2, DATES, 3, SUB, columns), f32),
            pltpu.VMEM((DATES, ROWS, 2 * columns), f32),
            pltpu.VMEM((2, GROUPS, SUB, columns), f32),
            pltpu.VMEM((DATES, 2, ROWS, columns), bf16),
            pltpu.SemaphoreType.DMA((7,)),
        ] + [sems] * 6,
        compiler_params=pltpu.CompilerParams(
            collective_id=0, has_side_effects=True, vmem_limit_bytes=60 * 1024 * 1024
        ),
        name="link",
    )(ref_date, halo, slcs, band, wide, dct)
    return (spectrum.astype(jnp.float32), compressed)


def solution(mesh):
    return jax.shard_map(
        on_device,
        mesh=mesh,
        in_specs=(P(None, ("grp", "pix"), None), P("grp")),
        out_specs=(P(None, ("grp", "pix"), None), P(None, None, ("grp", "pix"))),
        check_vma=False,
    )
```

time: 66.3 us -> 65.5 us (0.988)
  the two profiles are of different devices: /device:TPU:15 before, /device:TPU:0 now
where the time goes in v2:
time: 65.5 us; the launch traced here: 64.5 us
  Pallas kernels  57.5 us (88%)
  local copies, waits for them, and re-layouts  3.51 us (5%)
  other arithmetic  2.25 us (3%)
  between operations  1.33 us (2%)
    pallas_call x1, Pallas kernels, on_device(): pl.pallas_call(functools.partial(link_kernel, devices), out_shape=(jax.Sh...  57.5 us
    convert_element_type x1, other arithmetic, on_device(): return (spectrum.astype(jnp.float32), compressed)  2.15 us
    unnamed x4, local copies, waits for them, and re-layouts  2.15 us

profile of v2, /device:TPU:0, one launch (start us, length us, event | category | flops | bytes accessed | tf_op | source)
XLA Modules:
  0.0 64.5 jit_solution(17708659577595243978)
XLA Ops:
  1.3 0.1 pad.4.clone
  1.4 1.5 %copy.11 = bf16[2,64,2048]{1,2,0:T(8,128)(2,1)S(1)} copy(bf16[2,64,2048]{2,1,0:T(8,128)(2,1)} %x_ref.1) | data formatting | bytes 1048576 | tf_op args[0]
  2.9 0.1 fusion.4
  3.0 0.3 copy.14
  3.3 1.0 %reshape.15.h_ref = bf16[16,16,128]{2,1,0:T(8,128)(2,1)} reshape(bf16[16,2,8,8,16]{4,3,2,1,0:T(8,128)(2,1)S(1)} %bitcast.6) | data formatting | bytes 131072 | tf_op jit(solution)/shard_map/reshape | solution.py:377
  4.3 57.5 %link.1 = (bf16[2,64,2048]{2,1,0:T(8,128)(2,1)}, f32[2,64,128]{2,1,0:T(8,128)}) custom-call(s32[1]{0:T(128)S(6)} %copy.16.ref_ref, bf16[16,16,128]{2,1,0:T(8,128)(2,1)} %reshape.15.h_ref, bf16[2,64,2048]{2,1,0:T(8,128)(2,1)} %x_ref.1, bf16[256,128]{1,0:T(8,128)(2,1)} %constant.5.clone.band_ref, bf16[4,256,256]{2,1,0:T(8,128)(2,1)} %constant.3.clone.wide_ref, ...), custom_call_target="tpu_custom_call" | custom-call | tf_op jit(solution)/shard_map/link/pallas_call | solution.py:387
  61.8 0.0 copy-start
  61.8 2.1 %convert_element_type.3 = f32[2,64,2048]{2,1,0:T(8,128)} convert(bf16[2,64,2048]{2,1,0:T(8,128)(2,1)} %get-tuple-element.4) | non-fusion elementwise | flops 262144 | bytes 1572864 | tf_op jit(solution)/shard_map/convert_element_type | solution.py:422
  63.9 0.0 copy-done
  63.9 0.6 copy.17
  (2 shorter events, 0.0 us)
Async XLA Ops:
  61.8 2.2 %copy-start = (f32[2,64,128]{2,1,0:T(8,128)S(1)}, f32[2,64,128]{2,1,0:T(8,128)}, u32[]{:S(2)}) copy-start(f32[2,64,128]{2,1,0:T(8,128)} %get-tuple-element.11) | copy-start | bytes 196612

commit v3 on v2

--- a/solution.py
+++ b/solution.py
@@ -68,6 +68,14 @@
     return real, imag
 
 
+def exclusive_or(a, b, size):
+    total, bit = 0, 1
+    while bit < size:
+        total = total + ((a // bit + b // bit) % 2) * bit
+        bit *= 2
+    return total
+
+
 def chunk_index(p):
     whole, rest = p // CHUNK, p % CHUNK
     return (whole + 1) * (whole * (CHUNK // 2) + rest)
@@ -97,7 +105,7 @@
     barrier = pltpu.get_barrier_semaphore()
     for off in range(1, devices):
         pl.semaphore_signal(
-            barrier, inc=1, device_id={"pix": lax.rem(me + off, devices)}, device_id_type=MESH
+            barrier, inc=1, device_id={"pix": exclusive_or(me, off, devices)}, device_id_type=MESH
         )
 
     first_column = me * columns
@@ -116,14 +124,14 @@
         return xs.at[:, :, pl.ds(pl.multiple_of(n * columns, columns), columns)]
 
     def main_copy(off):
-        peer = lax.rem(me + off, devices)
+        peer = exclusive_or(me, off, devices)
         return pltpu.make_async_remote_copy(
             src_ref=block(peer), dst_ref=win.at[me], send_sem=ssem.at[off], recv_sem=rsem.at[off],
             device_id={"pix": peer}, device_id_type=MESH,
         )
 
     def halo_copy(off):
-        peer = lax.rem(me + off, devices)
+        peer = exclusive_or(me, off, devices)
         return pltpu.make_async_remote_copy(
             src_ref=h_ref.at[peer], dst_ref=hwin.at[me], send_sem=hs.at[off],
             recv_sem=hr.at[off], device_id={"pix": peer}, device_id_type=MESH,
@@ -143,7 +151,7 @@
         c.wait()
 
     def date_at(p):
-        return lax.rem(my_date - p + DATES, DATES)
+        return exclusive_or(my_date, p, DATES)
 
     def prepare_halo(p, carry):
         for q in range(per_date):
@@ -194,7 +202,7 @@
     def covariances(p, carry):
         for q in range(per_date):
             source = date_at(p) * per_date + q
-            off = lax.rem(me - source + devices, devices)
+            off = exclusive_or(me, source, devices)
 
             @pl.when(off != 0)
             def _():
@@ -228,25 +236,25 @@
                 ]
                 for g in range(GROUPS):
                     real, imag = sums[0][g], sums[1][g]
-                    cov[p, n * CHUNK + q, 0, g] = real
-                    cov[p, n * CHUNK + q, 1, g] = real + imag
-                    cov[p, n * CHUNK + q, 2, g] = imag - real
+                    cov[g, p, n * CHUNK + q, 0] = real
+                    cov[g, p, n * CHUNK + q, 1] = real + imag
+                    cov[g, p, n * CHUNK + q, 2] = imag - real
             return carry
 
         lax.fori_loop(0, p // CHUNK + 1, chunk, 0)
         for g in range(GROUPS):
-            cov[p, p, 0, g] = cov[p, p, 0, g] + LOADING
+            cov[g, p, p, 0] = cov[g, p, p, 0] + LOADING
         return carry
 
     lax.fori_loop(0, DATES, covariances, 0)
 
-    ref = lax.rem(my_date - ref_ref[0] + DATES, DATES)
+    ref = exclusive_or(my_date, ref_ref[0], DATES)
 
     def solve(g, carry):
         for i in range(DATES):
             one, two = jnp.maximum(ref, i), jnp.minimum(ref, i)
-            real = cov[one, two, 0, g]
-            imag = 0.5 * (cov[one, two, 1, g] + cov[one, two, 2, g])
+            real = cov[g, one, two, 0]
+            imag = 0.5 * (cov[g, one, two, 1] + cov[g, one, two, 2])
             sign = jnp.where(ref == i, 0.0, jnp.where(ref < i, 1.0, -1.0))
             imag = imag * sign
             vec[0, i, 0] = real
@@ -262,15 +270,22 @@
                     for q in range(SPAN):
                         i = base + q
                         one, two = max(i, j), min(i, j)
-                        cr = cov[one, two, 0, g]
+                        cr = cov[g, one, two, 0]
                         if i == j:
-                            terms = (cr * vs, cr * vi, -(cr * vr))
+                            terms, minus = (cr * vs, cr * vi, cr * vr), (False, False, True)
                         elif i > j:
-                            terms = (cr * vs, cov[i, j, 1, g] * vi, cov[i, j, 2, g] * vr)
+                            terms = (cr * vs, cov[g, i, j, 1] * vi, cov[g, i, j, 2] * vr)
+                            minus = (False, False, False)
                         else:
-                            terms = (cr * vs, -(cov[j, i, 2, g] * vi), -(cov[j, i, 1, g] * vr))
+                            terms = (cr * vs, cov[g, j, i, 2] * vi, cov[g, j, i, 1] * vr)
+                            minus = (False, True, True)
                         for n in range(3):
-                            acc[q][n] = terms[n] if acc[q][n] is None else acc[q][n] + terms[n]
+                            if acc[q][n] is None:
+                                acc[q][n] = -terms[n] if minus[n] else terms[n]
+                            elif minus[n]:
+                                acc[q][n] = acc[q][n] - terms[n]
+                            else:
+                                acc[q][n] = acc[q][n] + terms[n]
                 for q in range(SPAN):
                     real, imag = acc[q][0] - acc[q][1], acc[q][0] + acc[q][2]
                     vec[1 - src, base + q, 0] = real
@@ -308,7 +323,7 @@
 
     def tile_copy(p, q):
         peer = date_at(p) * per_date + q
-        off = lax.rem(peer - me + devices, devices)
+        off = exclusive_or(me, peer, devices)
         return off, pltpu.make_async_remote_copy(
             src_ref=tile.at[p, :, q * local_rows:(q + 1) * local_rows, :], dst_ref=mine,
             send_sem=ts.at[off], recv_sem=tr.at[off],
@@ -329,16 +344,17 @@
                     tile.at[p, :, q * local_rows:(q + 1) * local_rows, :], mine, local.at[6]
                 ).start()
 
-    def transform(p, carry):
+    def transform(n, carry):
+        p = DATES - 1 - n
         high, low = split_halves(linked[p])
         both = jnp.concatenate([high, high, low], axis=0)
         got = jnp.dot(dct[...], both, preferred_element_type=jnp.float32).astype(tile.dtype)
         tile[p, 0] = got[:, 0:columns]
         tile[p, 1] = got[:, columns:2 * columns]
 
-        @pl.when(p > 0)
+        @pl.when(n > 0)
         def _():
-            send(p - 1)
+            send(p + 1)
 
         return carry
 
@@ -346,7 +362,7 @@
     for c in range(2):
         for g in range(GROUPS):
             comp_ref[c, pl.ds(g, SUB, stride=GROUPS), :] = comp[c, g]
-    send(DATES - 1)
+    send(0)
 
     for c in mains:
         c.wait_send()
@@ -355,7 +371,7 @@
     for off in range(1, devices):
         pltpu.make_async_remote_copy(
             src_ref=own_tile, dst_ref=mine, send_sem=ts.at[off], recv_sem=tr.at[off],
-            device_id={"pix": lax.rem(me + off, devices)}, device_id_type=MESH,
+            device_id={"pix": exclusive_or(me, off, devices)}, device_id_type=MESH,
         ).wait()
 
 
@@ -407,7 +423,7 @@
             pltpu.VMEM((2 * CHUNK * ROWS, 2 * columns), bf16),
             pltpu.VMEM((2 * CHUNK * ROWS, columns), f32),
             pltpu.VMEM((GROUPS, SUB, columns), f32),
-            pltpu.VMEM((DATES, DATES, 3, GROUPS, SUB, columns), f32),
+            pltpu.VMEM((GROUPS, DATES, DATES, 3, SUB, columns), f32),
             pltpu.VMEM((2, DATES, 3, SUB, columns), f32),
             pltpu.VMEM((DATES, ROWS, 2 * columns), f32),
             pltpu.VMEM((2, GROUPS, SUB, columns), f32),

time: 65.5 us -> 57.8 us (0.88); the launches traced: 64.5 us -> 57.5 us
  Pallas kernels: 57.5 us -> 50.5 us
    pallas_call x1, Pallas kernels: 57.5 us -> 50.5 us  [on_device(): pl.pallas_call(functools.partial(link_kernel, devices), out_shape=(jax.Sh...]
where the time goes in v3:
time: 57.8 us; the launch traced here: 57.5 us
  Pallas kernels  50.5 us (87%)
  local copies, waits for them, and re-layouts  3.51 us (6%)
  other arithmetic  2.25 us (4%)
  between operations  1.33 us (2%)
    pallas_call x1, Pallas kernels, on_device(): pl.pallas_call(functools.partial(link_kernel, devices), out_shape=(jax.Sh...  50.5 us
    convert_element_type x1, other arithmetic, on_device(): return (spectrum.astype(jnp.float32), compressed)  2.15 us
    unnamed x4, local copies, waits for them, and re-layouts  2.15 us

profile of v3, /device:TPU:0, one launch (start us, length us, event | category | flops | bytes accessed | tf_op | source)
XLA Modules:
  0.0 57.5 jit_solution(12479234657481056484)
XLA Ops:
  1.3 0.1 pad.4.clone
  1.4 1.5 %copy.11 = bf16[2,64,2048]{1,2,0:T(8,128)(2,1)S(1)} copy(bf16[2,64,2048]{2,1,0:T(8,128)(2,1)} %x_ref.1) | data formatting | bytes 1048576 | tf_op args[0]
  2.9 0.1 fusion.4
  3.0 0.3 copy.14
  3.3 1.0 %reshape.15.h_ref = bf16[16,16,128]{2,1,0:T(8,128)(2,1)} reshape(bf16[16,2,8,8,16]{4,3,2,1,0:T(8,128)(2,1)S(1)} %bitcast.6) | data formatting | bytes 131072 | tf_op jit(solution)/shard_map/reshape | solution.py:393
  4.3 50.5 %link.1 = (bf16[2,64,2048]{2,1,0:T(8,128)(2,1)}, f32[2,64,128]{2,1,0:T(8,128)}) custom-call(s32[1]{0:T(128)S(6)} %copy.16.ref_ref, bf16[16,16,128]{2,1,0:T(8,128)(2,1)} %reshape.15.h_ref, bf16[2,64,2048]{2,1,0:T(8,128)(2,1)} %x_ref.1, bf16[256,128]{1,0:T(8,128)(2,1)} %constant.5.clone.band_ref, bf16[4,256,256]{2,1,0:T(8,128)(2,1)} %constant.3.clone.wide_ref, ...), custom_call_target="tpu_custom_call" | custom-call | tf_op jit(solution)/shard_map/link/pallas_call | solution.py:403
  54.7 0.0 copy-start
  54.8 2.1 %convert_element_type.3 = f32[2,64,2048]{2,1,0:T(8,128)} convert(bf16[2,64,2048]{2,1,0:T(8,128)(2,1)} %get-tuple-element.4) | non-fusion elementwise | flops 262144 | bytes 1572864 | tf_op jit(solution)/shard_map/convert_element_type | solution.py:438
  56.9 0.0 copy-done
  56.9 0.6 %copy.17 = f32[2,64,128]{2,1,0:T(8,128)} copy(f32[2,64,128]{2,1,0:T(8,128)S(1)} %copy-done) | data formatting | bytes 131072
  (2 shorter events, 0.0 us)
Async XLA Ops:
  54.7 2.2 %copy-start = (f32[2,64,128]{2,1,0:T(8,128)S(1)}, f32[2,64,128]{2,1,0:T(8,128)}, u32[]{:S(2)}) copy-start(f32[2,64,128]{2,1,0:T(8,128)} %get-tuple-element.11) | copy-start | bytes 196612
